TPU v7x, 32 devices: a 4x2x2 block of a 4x4x8 slice. The times are simulated.
32 devices in a mesh: dp: 4 (over y, z), tp: 8 (over x, core).
Axes of the slice: x: 4, y: 2, z: 2, core: 2. Of those that a mesh axis runs over, the one named last changes fastest.
The devices are a block of a 4x4x8 slice.
Arguments:
- hidden: bfloat16 [65536, 1024], P(('dp', 'tp')), parts along dimension 0
- ln_gain: float32 [1024], replicated
- ln_bias: float32 [1024], replicated
- embed: bfloat16 [8192, 1024], P('tp')
- targets: int32 [65536], P(('dp', 'tp')), parts along dimension 0
- loss_mask: int32 [65536], P(('dp', 'tp')), parts along dimension 0
Outputs:
- output 1: float32 [65536], P(('dp', 'tp')), parts along dimension 0
- output 2: float32 [4], P('dp'), parts along dimension 0
- output 3: bfloat16 [65536, 1024], P(('dp', 'tp')), parts along dimension 0
- output 4: float32 [32768, 1024], P(('dp', 'tp')), parts along dimension 0
- output 5: float32 [4096], P('dp'), parts along dimension 0
- output 6: float32 [4096], P('dp'), parts along dimension 0
There are 4 independent parts. A program takes and returns all parts, laid end to end along the dimension named above; an argument that names none is the same for every part.
All inputs are finite; a program needn't handle non-finite values.
Results may differ from a plain program's by a relative error of at most 0.001.
Values are sent between devices in bfloat16 or wider.
A program may use at most 768 MiB of HBM per device.

v0:
```python
import jax
import jax.numpy as jnp
from jax import lax
from jax.sharding import PartitionSpec as P

LN_EPS = 1e-5


def layer_norm(hidden, ln_gain, ln_bias):
    h_f32 = hidden.astype(jnp.float32)
    centred = h_f32 - jnp.mean(h_f32, axis=-1, keepdims=True)
    inv_std = lax.rsqrt(jnp.mean(centred * centred, axis=-1, keepdims=True) + LN_EPS)
    x_hat = centred * inv_std
    return x_hat, inv_std, (x_hat * ln_gain + ln_bias).astype(jnp.bfloat16)


def norm_backward(d_normed, x_hat, inv_std, ln_gain):
    value_a6 = d_normed * ln_gain
    centre_term = jnp.mean(value_a6, axis=-1, keepdims=True)
    proj_term = jnp.mean(value_a6 * x_hat, axis=-1, keepdims=True)
    return (inv_std * (value_a6 - centre_term - x_hat * proj_term)).astype(jnp.bfloat16)


def solution(mesh):
    group = mesh.shape['tp']

    def body(hidden, ln_gain, ln_bias, embed, targets, loss_mask):
        tokens = hidden.shape[0]
        shard_vocab = embed.shape[0]
        rank = lax.axis_index('tp')
        x_hat, inv_std, normed = layer_norm(hidden, ln_gain, ln_bias)
        gathered = lax.all_gather(normed, 'tp', tiled=True)
        all_targets = lax.all_gather(targets, 'tp', tiled=True)
        all_weights = lax.all_gather(loss_mask, 'tp', tiled=True).astype(jnp.float32)
        count = lax.psum(jnp.sum(loss_mask.astype(jnp.float32)), 'tp')
        logits = jnp.einsum('sd,vd->sv', gathered, embed, preferred_element_type=jnp.float32)
        vocab_ids = rank * shard_vocab + lax.broadcasted_iota(jnp.int32, (1, shard_vocab), 1)
        onehot = vocab_ids == all_targets[:, None]
        local_max = jnp.max(logits, axis=-1)
        local_sum = jnp.sum(jnp.exp(logits - local_max[:, None]), axis=-1)
        local_target = jnp.sum(jnp.where(onehot, logits, 0.0), axis=-1)
        global_max = lax.pmax(local_max, 'tp')
        combined = lax.psum(jnp.stack([local_sum * jnp.exp(local_max - global_max), local_target]), 'tp')
        log_norm = global_max + jnp.log(combined[0])
        all_loss = (log_norm - combined[1]) * all_weights
        mean_loss = jnp.sum(all_loss) / count
        d_logits = ((jnp.exp(logits - log_norm[:, None]) - onehot.astype(jnp.float32)) * (all_weights / count)[:, None]).astype(jnp.bfloat16)
        d_embed = jnp.einsum('sv,sd->vd', d_logits, gathered, preferred_element_type=jnp.float32)
        d_part = jnp.einsum('sv,vd->sd', d_logits, embed, preferred_element_type=jnp.float32)
        d_normed = lax.psum_scatter(d_part, 'tp', scatter_dimension=0, tiled=True)
        norm_grads = lax.psum(jnp.stack([jnp.sum(d_normed * x_hat, axis=0), jnp.sum(d_normed, axis=0)]), 'tp')
        d_hidden = norm_backward(d_normed, x_hat, inv_std, ln_gain)
        own_loss = all_loss.reshape(group, tokens)[rank]
        return own_loss, mean_loss.reshape(1), d_hidden, d_embed, norm_grads[0], norm_grads[1]

    token_rows = P(('dp', 'tp'))
    token_mat = P(('dp', 'tp'), None)
    return jax.shard_map(body, mesh=mesh, in_specs=(token_mat, P(), P(), P('tp', None), token_rows, token_rows), out_specs=(token_rows, P('dp'), token_mat, token_mat, P('dp'), P('dp')), check_vma=False)
```

profile of v0, /device:TPU:81, one launch (start us, length us, event | category | flops | bytes accessed | tf_op | source)
XLA Modules:
  0.0 771.7 jit_solution(16172377796602467502)
XLA Ops:
  7.2 0.1 all-gather.2.cloned.1.call-start
  7.3 3.0 convert_reduce_fusion
  10.3 3.0 fusion.17
  13.4 0.6 copy-done.6
  14.0 3.0 fusion.11
  17.0 0.1 all-gather.2.cloned.1.call-update
  17.0 0.1 all-reduce.3.cloned.1.call-start
  17.1 14.8 %all_gather.10 = s32[16384]{0:T(1024)S(1)} all-gather(s32[2048]{0:T(1024)S(1)} %copy-done.11), channel_id=1, replica_groups=mesh['dp'=4,'tp'=8] {'tp'}, dimensions={0}, use_global_device_ids=true | all-gather | bytes 73728 | tf_op jit(solution)/shard_map/all_gather | solution.py:33
  31.9 143.4 %all-gather.2.cloned.1.call-done = bf16[16384,1024]{1,0:T(8,128)(2,1)} async-done(((bf16[2048,1024]{1,0:T(8,128)(2,1)}), bf16[16384,1024]{1,0:T(8,128)(2,1)}) %all-gather.2.cloned.1.call-update) | async-done | bytes 33554448 | tf_op jit(solution)/shard_map/all_gather | solution.py:32
  175.4 45.8 %fusion.20 = (f32[16384]{0:T(1024)}, f32[16384,1024]{0,1:T(8,128)}) fusion(bf16[16384,1024]{1,0:T(8,128)(2,1)} %all-gather.2.cloned.1.call-done, bf16[1024,1024]{1,0:T(8,128)(2,1)S(1)} %copy-done), kind=kOutput, calls=%fused_computation.39 | convolution fusion | flops 34376499200 | bytes 102825984 | tf_op jit(solution)/shard_map/sd,vd->sv/dot_general | solution.py:36
  221.2 0.1 all-reduce.3.cloned.1.call-update
  221.2 0.2 all-reduce.5.cloned.1.call-start
  221.5 26.1 %exponential_reduce_fusion = (f32[16384]{0:T(1024)S(1)}, f32[16384]{0:T(1024)S(1)}) fusion(f32[16384,1024]{0,1:T(8,128)} %get-tuple-element.21, f32[16384]{0:T(1024)} %get-tuple-element.20, s32[16384]{0:T(1024)S(1)} %all_gather.10, s32[1024]{0:T(1024)S(1)} %iota_add_fusion), kind=kLoop, calls=%fused_computation.6 | loop fusion | flops 83853312 | bytes 67375104 | tf_op jit(solution)/shard_map/reduce_sum | solution.py:40
  247.6 25.5 %all-reduce.3.cloned.1.call-done = f32[16384]{0:T(1024)} async-done(((f32[16384]{0:T(1024)}), f32[16384]{0:T(1024)}) %all-reduce.3.cloned.1.call-update) | async-done | bytes 65552 | tf_op jit(solution)/shard_map/pmax | solution.py:42
  273.1 0.9 exponential_multiply_fusion
  273.9 0.8 pad_maximum_fusion
  274.8 0.1 reduce-scatter.2.cloned.1.call-start
  274.9 0.6 convert_reduce_fusion.1
  275.5 15.4 %psum.22 = f32[]{:T(128)} all-reduce(f32[]{:T(128)} %convert_reduce_fusion.1), channel_id=1, replica_groups=mesh['dp'=4,'tp'=8] {'tp'}, use_global_device_ids=true, to_apply=%region_9.10 | all-reduce | flops 1 | bytes 8 | tf_op jit(solution)/shard_map/psum | solution.py:35
  290.9 14.0 %all_gather.11 = s32[16384]{0:T(1024)S(1)} all-gather(s32[2048]{0:T(1024)S(1)} %copy-done.10), channel_id=1, replica_groups=mesh['dp'=4,'tp'=8] {'tp'}, dimensions={0}, use_global_device_ids=true | all-gather | bytes 73728 | tf_op jit(solution)/shard_map/all_gather | solution.py:34
  304.9 23.9 %all-reduce.5.cloned.1.call-done = f32[2,16384]{1,0:T(2,128)} async-done(((f32[2,16384]{1,0:T(2,128)}), f32[2,16384]{1,0:T(2,128)}) %all-reduce.5.cloned.1.call-update) | async-done | bytes 131088 | tf_op jit(solution)/shard_map/psum | solution.py:43
  328.7 1.1 slice_log_fusion
  329.9 2.1 fusion.18
  332.0 33.3 %fusion.3 = bf16[16384,1024]{0,1:T(8,128)(2,1)} fusion(f32[16384,1024]{0,1:T(8,128)} %get-tuple-element.21, f32[16384]{0:T(1024)S(1)} %get-tuple-element.17, f32[16384]{0:T(1024)S(1)} %get-tuple-element.14, s32[16384]{0:T(1024)S(1)} %all_gather.10, s32[1024]{0:T(1024)S(1)} %iota_add_fusion), kind=kLoop, calls=%fused_computation.5 | loop fusion | flops 100663296 | bytes 100864000 | tf_op jit(solution)/shard_map/convert_element_type | solution.py:47
  365.3 45.6 %fusion.21 = f32[16384,1024]{1,0:T(8,128)} fusion(bf16[16384,1024]{0,1:T(8,128)(2,1)} %fusion.3, bf16[1024,1024]{1,0:T(8,128)(2,1)S(1)} %copy-done), kind=kOutput, calls=%fused_computation.40 | convolution fusion | flops 34359738368 | bytes 102760448 | tf_op jit(solution)/shard_map/sv,vd->sd/dot_general | solution.py:49
  412.4 0.6 constant_dynamic-slice_fusion
  413.0 41.9 %fusion.22 = f32[1024,1024]{1,0:T(8,128)} fusion(bf16[16384,1024]{0,1:T(8,128)(2,1)} %fusion.3, bf16[16384,1024]{1,0:T(8,128)(2,1)} %all-gather.2.cloned.1.call-done), kind=kOutput, calls=%fused_computation.41 | convolution fusion | flops 34359738368 | bytes 71303168 | tf_op jit(solution)/shard_map/sv,sd->vd/dot_general | solution.py:48
  454.9 281.7 %reduce-scatter.2.cloned.1.call-done = f32[2048,1024]{1,0:T(8,128)} async-done(((f32[16384,1024]{1,0:T(8,128)}), f32[2048,1024]{1,0:T(8,128)}) %reduce-scatter.2.cloned.1.call-update) | async-done | bytes 8388624 | tf_op jit(solution)/shard_map/reduce_scatter | solution.py:50
  736.6 6.3 fusion.16
  743.0 13.1 %psum.23 = f32[2,1024]{1,0:T(2,128)S(1)} all-reduce(f32[2,1024]{1,0:T(2,128)S(1)} %pad_maximum_fusion.1), channel_id=1, replica_groups=mesh['dp'=4,'tp'=8] {'tp'}, use_global_device_ids=true, to_apply=%region_15.16 | all-reduce | flops 2048 | bytes 16384 | tf_op jit(solution)/shard_map/psum | solution.py:51
  756.1 0.6 fusion.19
  756.7 7.3 fusion.15
  (33 shorter events, 0.2 us)
Async XLA Ops:
  7.2 168.2 %copy-start = (bf16[1024,1024]{1,0:T(8,128)(2,1)S(1)}, bf16[1024,1024]{1,0:T(8,128)(2,1)}, u32[]{:S(2)}) copy-start(bf16[1024,1024]{1,0:T(8,128)(2,1)} %param.9) | copy-start | bytes 6291460
  7.2 6.8 copy-start.8
  7.2 6.8 copy-start.12
  7.2 168.2 %all-gather.2.cloned.1.call-start = ((), (), s32[]{:S(2)}) async-start(), calls=%async_computation.1 | async-start | bytes 37748736 | tf_op jit(solution)/shard_map/all_gather | solution.py:32
  7.3 6.7 copy-start.2
  10.3 3.1 copy-start.4
  10.3 6.8 copy-start.11
  13.4 0.6 copy-start.6
  17.0 256.1 %all-reduce.3.cloned.1.call-start = ((), (), s32[]{:S(2)}) async-start(), calls=%async_computation.2 | async-start | bytes 131072 | tf_op jit(solution)/shard_map/pmax | solution.py:42
  221.2 107.5 %all-reduce.5.cloned.1.call-start = ((), (), s32[]{:S(2)}) async-start(), calls=%async_computation.3 | async-start | bytes 262144 | tf_op jit(solution)/shard_map/psum | solution.py:43
  221.5 51.6 %copy-start.3 = (f32[16384]{0:T(1024)S(1)}, f32[16384]{0:T(1024)}, u32[]{:S(2)}) copy-start(f32[16384]{0:T(1024)} %get-tuple-element.20) | copy-start | bytes 196612
  221.5 53.4 %copy-start.10 = (s32[2048]{0:T(1024)S(1)}, s32[2048]{0:T(1024)}, u32[]{:S(2)}) copy-start(s32[2048]{0:T(1024)} %param.11) | copy-start | bytes 24580
  274.8 461.8 %reduce-scatter.2.cloned.1.call-start = ((), (), s32[]{:S(2)}) async-start(), calls=%async_computation.4 | async-start | bytes 75497472 | tf_op jit(solution)/shard_map/reduce_scatter | solution.py:50
  413.0 323.6 %copy-start.5 = (f32[2048]{0:T(1024)S(1)}, f32[2048]{0:T(1024)}, u32[]{:S(2)}) copy-start(f32[2048]{0:T(1024)} %copy-done.4) | copy-start | bytes 24580
  413.0 323.6 %copy-start.7 = (f32[2048]{0:T(1024)S(1)}, f32[2048]{0:T(1024)}, u32[]{:S(2)}) copy-start(f32[2048]{0:T(1024)} %copy-done.6) | copy-start | bytes 24580
  413.0 323.6 %copy-start.9 = (f32[1024]{0:T(1024)S(1)}, f32[1024]{0:T(1024)}, u32[]{:S(2)}) copy-start(f32[1024]{0:T(1024)} %param.7) | copy-start | bytes 12292
  756.7 7.3 copy-start.1
Sparse Core Ops, SparseCore 0:
  17.1 158.1 all-gather.1
  221.3 51.6 all-reduce.2
  276.0 52.6 all-reduce.4
  411.1 325.4 reduce-scatter.1
where the time goes:
time: 772 us
  waiting for transfers between devices  475 us (62%)
  matrix products  133 us (17%)
  other arithmetic  86.5 us (11%)
  blocking collectives  57.4 us (7%)
  between operations  16.4 us (2%)
    reduce_scatter x1, waiting for transfers between devices, body(): d_normed = lax.psum_scatter(d_part, 'tp', scatter_dimension=0, tiled=True)  282 us
    all_gather x1, waiting for transfers between devices, body(): gathered = lax.all_gather(normed, 'tp', tiled=True)  143 us
    dot_general x1, matrix products, body(): jnp.einsum('sd,vd->sv', gathered, embed, preferred_element_type=jnp.float32)  45.8 us
    dot_general x1, matrix products, body(): jnp.einsum('sv,vd->sd', d_logits, embed, preferred_element_type=jnp.float32)  45.6 us
    dot_general x1, matrix products, body(): jnp.einsum('sv,sd->vd', d_logits, gathered, preferred_element_type=jnp.fl...  41.9 us
    convert_element_type x1, other arithmetic, body(): ((jnp.exp(logits - log_norm[:, None]) - onehot.astype(jnp.float32)) * (al...  33.3 us
    reduce_sum x1, other arithmetic, body(): local_sum = jnp.sum(jnp.exp(logits - local_max[:, None]), axis=-1)  26.1 us
    pmax x1, waiting for transfers between devices, body(): global_max = lax.pmax(local_max, 'tp')  25.5 us
  transfers between devices with their start and end apart: 4, of which 4 were waited for; matrix products, arithmetic and copies ran while one was open for 9% of the time, Pallas kernels for 0%

commit v1 on v0

v1 whole, which is shorter than its diff:
```python
import jax
import jax.numpy as jnp
from jax import lax
from jax.sharding import PartitionSpec as P

LN_EPS = 1e-5


def layer_norm(hidden, ln_gain, ln_bias):
    h_f32 = hidden.astype(jnp.float32)
    centred = h_f32 - jnp.mean(h_f32, axis=-1, keepdims=True)
    inv_std = lax.rsqrt(jnp.mean(centred * centred, axis=-1, keepdims=True) + LN_EPS)
    x_hat = centred * inv_std
    return x_hat, inv_std, (x_hat * ln_gain + ln_bias).astype(jnp.bfloat16)


def norm_backward(d_normed, x_hat, inv_std, ln_gain):
    scaled = d_normed * ln_gain
    centre_term = jnp.mean(scaled, axis=-1, keepdims=True)
    proj_term = jnp.mean(scaled * x_hat, axis=-1, keepdims=True)
    return (inv_std * (scaled - centre_term - x_hat * proj_term)).astype(jnp.bfloat16)


def solution(mesh):
    def body(hidden, ln_gain, ln_bias, embed, targets, loss_mask):
        table = lax.all_gather(embed, 'tp', tiled=True)
        weights = loss_mask.astype(jnp.float32)
        count = lax.psum(jnp.sum(weights), 'tp')
        x_hat, inv_std, normed = layer_norm(hidden, ln_gain, ln_bias)
        logits = jnp.einsum('sd,vd->sv', normed, table, preferred_element_type=jnp.float32)
        onehot = lax.broadcasted_iota(jnp.int32, (1, table.shape[0]), 1) == targets[:, None]
        row_max = jnp.max(logits, axis=-1)
        row_sum = jnp.sum(jnp.exp(logits - row_max[:, None]), axis=-1)
        t_logit = jnp.sum(jnp.where(onehot, logits, 0.0), axis=-1)
        log_norm = row_max + jnp.log(row_sum)
        loss = (log_norm - t_logit) * weights
        d_logits = ((jnp.exp(logits - log_norm[:, None]) - onehot.astype(jnp.float32)) * (weights / count)[:, None]).astype(jnp.bfloat16)
        d_embed_part = jnp.einsum('sv,sd->vd', d_logits, normed, preferred_element_type=jnp.float32)
        d_embed = lax.psum_scatter(d_embed_part, 'tp', scatter_dimension=0, tiled=True)
        d_normed = jnp.einsum('sv,vd->sd', d_logits, table, preferred_element_type=jnp.float32)
        sums = jnp.concatenate([jnp.sum(d_normed * x_hat, axis=0), jnp.sum(d_normed, axis=0), jnp.full((128,), jnp.sum(loss))])
        sums = lax.psum(sums, 'tp')
        dim = hidden.shape[1]
        mean_loss = sums[2 * dim:2 * dim + 1] / count
        d_hidden = norm_backward(d_normed, x_hat, inv_std, ln_gain)
        return loss, mean_loss, d_hidden, d_embed, sums[:dim], sums[dim:2 * dim]

    token_rows = P(('dp', 'tp'))
    token_mat = P(('dp', 'tp'), None)
    return jax.shard_map(body, mesh=mesh, in_specs=(token_mat, P(), P(), P('tp', None), token_rows, token_rows), out_specs=(token_rows, P('dp'), token_mat, token_mat, P('dp'), P('dp')), check_vma=False)
```

time: 772 us -> 425 us (0.55)
  waiting for transfers between devices: 475 us -> 156 us
  blocking collectives: 57.4 us -> 35.9 us
  other arithmetic: 86.5 us -> 75.4 us
    reduce_scatter x1, waiting for transfers between devices: 282 us -> 88.9 us  [body(): lax.psum_scatter(d_embed_part, 'tp', scatter_dimension=0, tiled=True)]
    all_gather x1, waiting for transfers between devices: 143 us -> 66.7 us  [body(): table = lax.all_gather(embed, 'tp', tiled=True)]
    all_gather x2 -> x0, blocking collectives: 28.8 us -> none  [the longest x1 14.8 us: body(): all_targets = lax.all_gather(targets, 'tp', tiled=True)]
    pmax x1 -> x0, waiting for transfers between devices: 25.5 us -> none  [body(): global_max = lax.pmax(local_max, 'tp')]
    psum x1 -> x0, waiting for transfers between devices: 23.9 us -> none  [body(): lax.psum(jnp.stack([local_sum * jnp.exp(local_max - global_max), local_ta...]
    reduce_sum x4 -> x3, other arithmetic: 35.2 us -> 28.9 us  [the longest x1 25.8 us: body(): t_logit = jnp.sum(jnp.where(onehot, logits, 0.0), axis=-1)]
    convert_element_type x3 -> x2, other arithmetic: 43.6 us -> 40.7 us  [the longest x1 33.5 us: body(): ((jnp.exp(logits - log_norm[:, None]) - onehot.astype(jnp.float32)) * (we...]
  transfers between devices with their start and end apart: 4 -> 2, of which waited for: 4 -> 2; matrix products, arithmetic and copies ran while one was open for 9% -> 15% of each run, Pallas kernels for 0% -> 0%
where the time goes in v1:
time: 425 us
  waiting for transfers between devices  156 us (37%)
  matrix products  139 us (33%)
  other arithmetic  75.4 us (18%)
  blocking collectives  35.9 us (8%)
  between operations  16.6 us (4%)
    reduce_scatter x1, waiting for transfers between devices, body(): lax.psum_scatter(d_embed_part, 'tp', scatter_dimension=0, tiled=True)  88.9 us
    all_gather x1, waiting for transfers between devices, body(): table = lax.all_gather(embed, 'tp', tiled=True)  66.7 us
    dot_general x1, matrix products, body(): jnp.einsum('sd,vd->sv', normed, table, preferred_element_type=jnp.float32)  47.1 us
    dot_general x1, matrix products, body(): jnp.einsum('sv,vd->sd', d_logits, table, preferred_element_type=jnp.float32)  46.8 us
    dot_general x1, matrix products, body(): jnp.einsum('sv,sd->vd', d_logits, normed, preferred_element_type=jnp.floa...  44.9 us
    convert_element_type x1, other arithmetic, body(): ((jnp.exp(logits - log_norm[:, None]) - onehot.astype(jnp.float32)) * (we...  33.5 us
    reduce_sum x1, other arithmetic, body(): t_logit = jnp.sum(jnp.where(onehot, logits, 0.0), axis=-1)  25.8 us
    psum x1, blocking collectives, body(): sums = lax.psum(sums, 'tp')  21.5 us
  transfers between devices with their start and end apart: 2, of which 2 were waited for; matrix products, arithmetic and copies ran while one was open for 15% of the time, Pallas kernels for 0%

profile of v1, /device:TPU:81, one launch (start us, length us, event | category | flops | bytes accessed | tf_op | source)
XLA Modules:
  0.0 425.0 jit_solution(17927266203801899880)
XLA Ops:
  7.2 0.0 copy-start.3
  7.2 0.0 copy-start.2
  7.2 0.1 all-gather.2.cloned.1.call-start
  7.3 0.7 all-gather.2.cloned.1.call-update
  8.0 0.1 reduce-scatter.2.cloned.1.call-start
  8.1 1.3 convert_reduce_fusion.1
  9.4 14.4 %psum.14 = f32[]{:T(128)} all-reduce(f32[]{:T(128)} %convert_reduce_fusion.1), channel_id=1, replica_groups=mesh['dp'=4,'tp'=8] {'tp'}, use_global_device_ids=true, to_apply=%region_6.7 | all-reduce | flops 1 | bytes 8 | tf_op jit(solution)/shard_map/psum | solution.py:28
  23.8 2.8 convert_reduce_fusion
  26.6 3.0 fusion.13
  29.6 0.0 copy-start.1
  29.6 66.7 %all-gather.2.cloned.1.call-done = bf16[8192,1024]{1,0:T(8,128)(2,1)} async-done(((bf16[1024,1024]{1,0:T(8,128)(2,1)}), bf16[8192,1024]{1,0:T(8,128)(2,1)}) %all-gather.2.cloned.1.call-update) | async-done | bytes 16777232 | tf_op jit(solution)/shard_map/all_gather | solution.py:26
  96.3 0.0 copy-done.3
  96.3 0.0 copy-done.2
  96.3 47.1 %fusion.20 = (f32[2048]{0:T(1024)S(1)}, f32[2048,8192]{1,0:T(8,128)}) fusion(bf16[8192,1024]{1,0:T(8,128)(2,1)} %all-gather.2.cloned.1.call-done, bf16[2048,1024]{1,0:T(8,128)(2,1)} %param.6, f32[1024]{0:T(1024)S(1)} %copy-done.3, f32[1024]{0:T(1024)S(1)} %copy-done.2, f32[2048]{0:T(1024)S(1)} %add_rsqrt_fusion, f32[2048]{0:T(1024)S(1)} %broadcast_multiply_fusion.2), kind=kOutput, calls=%fused_computation.34 | convolution fusion | flops 34389098496 | bytes 88113152 | tf_op jit(solution)/shard_map/sd,vd->sv/dot_general | solution.py:30
  143.4 0.0 copy-done.1
  143.4 0.0 copy-start
  143.4 25.8 %select_reduce_fusion = (f32[2048]{0:T(1024)S(1)}, f32[2048]{0:T(1024)S(1)}) fusion(f32[2048,8192]{1,0:T(8,128)} %get-tuple-element.19, s32[2048]{0:T(1024)S(1)} %copy-done.1, f32[2048]{0:T(1024)S(1)} %get-tuple-element.18), kind=kLoop, calls=%fused_computation.1 | loop fusion | flops 83881984 | bytes 67141632 | tf_op jit(solution)/shard_map/reduce_sum | solution.py:34
  169.2 0.0 copy-done
  169.2 1.9 fusion.18
  171.1 33.5 %multiply_convert_fusion = bf16[2048,8192]{1,0:T(8,128)(2,1)} fusion(f32[2048,8192]{1,0:T(8,128)} %get-tuple-element.19, f32[2048]{0:T(1024)S(1)} %get-tuple-element.17, f32[2048]{0:T(1024)S(1)} %get-tuple-element.14, s32[2048]{0:T(1024)S(1)} %copy-done.1), kind=kLoop, calls=%fused_computation | loop fusion | flops 100663296 | bytes 100687872 | tf_op jit(solution)/shard_map/convert_element_type | solution.py:37
  204.5 44.9 %fusion.14 = f32[8192,1024]{1,0:T(8,128)} fusion(bf16[2048,8192]{1,0:T(8,128)(2,1)} %multiply_convert_fusion, bf16[2048,1024]{1,0:T(8,128)(2,1)} %param.6, f32[1024]{0:T(1024)S(1)} %copy-done.3, f32[1024]{0:T(1024)S(1)} %copy-done.2, f32[2048]{0:T(1024)S(1)} %add_rsqrt_fusion, f32[2048]{0:T(1024)S(1)} %broadcast_multiply_fusion.2), kind=kOutput, calls=%fused_computation.30 | convolution fusion | flops 34372321280 | bytes 71327744 | tf_op jit(solution)/shard_map/sv,sd->vd/dot_general | solution.py:38
  249.4 0.1 reduce-scatter.2.cloned.1.call-update
  249.5 46.8 %fusion.9 = (f32[2048]{0:T(1024)S(1)}, f32[1024]{0:T(1024)S(1)}, f32[2048]{0:T(1024)S(1)}, f32[1024]{0:T(1024)S(1)}, f32[2048,1024]{1,0:T(8,128)}) fusion(bf16[2048,1024]{1,0:T(8,128)(2,1)} %param.6, f32[1024]{0:T(1024)S(1)} %copy-done.2, f32[2048]{0:T(1024)S(1)} %add_rsqrt_fusion, f32[2048]{0:T(1024)S(1)} %broadcast_multiply_fusion.2, ...), kind=kOutput, calls=%fused_computation.15 | convolution fusion | flops 34380709888 | bytes 62959616 | tf_op jit(solution)/shard_map/sv,vd->sd/dot_general | solution.py:40
  296.3 0.6 broadcast_in_dim.6
  297.0 21.5 %psum.15 = f32[2176]{0:T(1024)S(1)} all-reduce(f32[2176]{0:T(1024)S(1)} %pad_maximum_fusion), channel_id=1, replica_groups=mesh['dp'=4,'tp'=8] {'tp'}, use_global_device_ids=true, to_apply=%region_10.11 | all-reduce | flops 2176 | bytes 17408 | tf_op jit(solution)/shard_map/psum | solution.py:42
  318.4 0.5 slice.12
  320.3 0.6 fusion.19
  320.9 7.2 %fusion.12 = bf16[2048,1024]{1,0:T(8,128)(2,1)} fusion(bf16[2048,1024]{1,0:T(8,128)(2,1)} %param.6, f32[2048,1024]{1,0:T(8,128)} %get-tuple-element.20, f32[2048]{0:T(1024)S(1)} %get-tuple-element.21, f32[2048]{0:T(1024)S(1)} %get-tuple-element.22, f32[1024]{0:T(1024)S(1)} %copy-done.2, f32[2048]{0:T(1024)S(1)} %add_rsqrt_fusion, ...), kind=kLoop, calls=%fused_computation.18 | loop fusion | flops 18874368 | bytes 16814080 | tf_op jit(solution)/shard_map/convert_element_type | solution.py:21
  328.1 88.9 %reduce-scatter.2.cloned.1.call-done = f32[1024,1024]{1,0:T(8,128)} async-done(((f32[8192,1024]{1,0:T(8,128)}), f32[1024,1024]{1,0:T(8,128)}) %reduce-scatter.2.cloned.1.call-update) | async-done | bytes 4194320 | tf_op jit(solution)/shard_map/reduce_scatter | solution.py:39
  (4 shorter events, 0.0 us)
Async XLA Ops:
  7.2 89.1 %copy-start.3 = (f32[1024]{0:T(1024)S(1)}, f32[1024]{0:T(1024)}, u32[]{:S(2)}) copy-start(f32[1024]{0:T(1024)} %param.8) | copy-start | bytes 12292
  7.2 89.1 %copy-start.2 = (f32[1024]{0:T(1024)S(1)}, f32[1024]{0:T(1024)}, u32[]{:S(2)}) copy-start(f32[1024]{0:T(1024)} %param.7) | copy-start | bytes 12292
  7.2 89.1 %all-gather.2.cloned.1.call-start = ((), (), s32[]{:S(2)}) async-start(), calls=%async_computation.1 | async-start | bytes 18874368 | tf_op jit(solution)/shard_map/all_gather | solution.py:26
  8.0 409.0 %reduce-scatter.2.cloned.1.call-start = ((), (), s32[]{:S(2)}) async-start(), calls=%async_computation.2 | async-start | bytes 37748736 | tf_op jit(solution)/shard_map/reduce_scatter | solution.py:39
  29.6 113.8 %copy-start.1 = (s32[2048]{0:T(1024)S(1)}, s32[2048]{0:T(1024)}, u32[]{:S(2)}) copy-start(s32[2048]{0:T(1024)} %param.10) | copy-start | bytes 24580
  143.4 25.8 %copy-start = (s32[2048]{0:T(1024)S(1)}, s32[2048]{0:T(1024)}, u32[]{:S(2)}) copy-start(s32[2048]{0:T(1024)} %param.11) | copy-start | bytes 24580
Sparse Core Ops, SparseCore 0:
  9.7 86.6 all-gather.1
  249.6 167.3 reduce-scatter.1

commit v2 on v1

v2 whole, which is shorter than its diff:
```python
import functools

import jax
import jax.numpy as jnp
from jax import lax
from jax.experimental import pallas as pl
from jax.experimental.pallas import tpu as pltpu
from jax.sharding import PartitionSpec as P

LN_EPS = 1e-5
LANES = 128
PIECE = 256
TILE = 512
MESH = pl.DeviceIdType.MESH
F32 = jnp.float32
BF16 = jnp.bfloat16


def matmul_t(a, b):
    return lax.dot_general(a, b, (((1,), (1,)), ((), ())), preferred_element_type=F32)


def matmul(a, b):
    return jnp.dot(a, b, preferred_element_type=F32)


def widen(col, width):
    return jnp.concatenate([col] * (width // LANES), axis=1)


def to_row(col):
    return jnp.transpose(jnp.broadcast_to(col, (LANES, LANES)))[0:1, :]


def to_col(row):
    return jnp.transpose(jnp.broadcast_to(row, (LANES, LANES)))


def kernel(n, hidden, gain, bias, embed, tgt, msk,
           loss_o, mean_o, dh_o, de_o, dg_o, db_o, z_h, x_h,
           e_all, x_own, hid, de_acc, max_s, sum_s, mu_s, rs_s, xbuf, dz_a, dz_b, zb, dx_acc, zt,
           tcol, wcol, tg_all, mk_all, ls_all, sm_all, gb, inv_s,
           e_send, e_recv, ep_send, ep_recv, e_pair, x_send, x_recv, xp_send, xp_recv, x_pair,
           tg_sem, mk_sem, ls_sem, sm_sem, hid_sem, loc_sem, z_sem, zl_sem, xl_sem, dh_sem):
    tokens, dim = hid.shape
    shard = embed.shape[0]
    chips = n // 2
    e_parts, x_parts = shard // PIECE, tokens // PIECE
    e_rounds, x_rounds = e_parts + e_parts // 2, x_parts + x_parts // 2
    blocks = tokens // LANES
    tiles = tokens // TILE
    me = lax.axis_index('tp')
    chip, core = me // 2, me % 2
    partner = 2 * chip + 1 - core
    right, left = (me + 2) % n, (me + n - 2) % n
    ring_dev = (right, left)

    def remote(src, dst, ssem, rsem, dev):
        return pltpu.make_async_remote_copy(src_ref=src, dst_ref=dst, send_sem=ssem, recv_sem=rsem,
                                            device_id={'tp': dev}, device_id_type=MESH)

    def piece(buf, slot, q):
        return buf.at[slot, pl.ds(pl.multiple_of(q * PIECE, PIECE), PIECE), :]

    def ring_src(j, d, parts):
        off = (2 * d - 1) * (j // parts)
        return 2 * ((chip + off + chips) % chips) + core, (j + d * (parts // 2)) % parts

    def arrival(j, d, parts, lane):
        off = (2 * d - 1) * (1 + j // parts)
        side = core + lane * (1 - 2 * core)
        return 2 * ((chip + off + chips) % chips) + side, (j + d * (parts // 2)) % parts

    def e_ring(j, d, src=None):
        slot, q = ring_src(j, d, e_parts)
        ref = piece(e_all, slot, q)
        if src is None:
            src = ref
        else:
            src = src.at[pl.ds(pl.multiple_of(q * PIECE, PIECE), PIECE), :]
        return remote(src, ref, e_send.at[d, j], e_recv.at[d, j], ring_dev[d])

    def e_relay(j, d, lane):
        slot, q = arrival(j, d, e_parts, lane)
        ref = piece(e_all, slot, q)
        return remote(ref, ref, ep_send.at[d, j], ep_recv.at[d, j], partner)

    def e_wait(j, d):
        slot, q = arrival(j, d, e_parts, 0)
        ref = piece(e_all, slot, q)
        remote(ref, ref, e_send.at[d, j], e_recv.at[d, j], ring_dev[d]).wait_recv()

    def x_ring(j, d):
        slot, q = ring_src(j, d, x_parts)
        ref = piece(x_h, slot, q)
        return remote(ref, ref, x_send.at[d, j], x_recv.at[d, j], ring_dev[d])

    def x_relay(j, d, lane):
        slot, q = arrival(j, d, x_parts, lane)
        ref = piece(x_h, slot, q)
        return remote(ref, ref, xp_send.at[d, j], xp_recv.at[d, j], partner)

    def x_wait(j, d):
        slot, q = arrival(j, d, x_parts, 0)
        ref = piece(x_h, slot, q)
        remote(ref, ref, x_send.at[d, j], x_recv.at[d, j], ring_dev[d]).wait_recv()

    def to_all(src, dst, sem):
        return [remote(src, dst, sem.at[0, d], sem.at[1, d], (me + d) % n) for d in range(1, n)]

    barrier = pltpu.get_barrier_semaphore()
    for d in range(1, n):
        pl.semaphore_signal(barrier, inc=1, device_id={'tp': (me + d) % n}, device_id_type=MESH)
    hid_copies = [pltpu.make_async_copy(hidden.at[pl.ds(t * TILE, TILE), :], hid.at[pl.ds(t * TILE, TILE), :], hid_sem.at[t]) for t in range(tiles)]
    for cp in hid_copies:
        cp.start()
    e_own = pltpu.make_async_copy(embed, e_all.at[me], loc_sem.at[0])
    e_own.start()
    pl.semaphore_wait(barrier, n - 1)

    tg_copies = to_all(tgt, tg_all.at[me], tg_sem)
    mk_copies = to_all(msk, mk_all.at[me], mk_sem)
    for cp in tg_copies + mk_copies:
        cp.start()
    for j in range(e_parts):
        for d in range(2):
            e_ring(j, d, embed).start()
    e_swap = remote(embed, e_all.at[me], e_pair.at[0], e_pair.at[1], partner)
    e_swap.start()

    tg_all[me] = tgt[...]
    mk_all[me] = msk[...]
    max_s[...] = jnp.full_like(max_s, -jnp.inf)
    sum_s[...] = jnp.zeros_like(sum_s)

    rows_ln = 64
    for t in range(tiles):
        hid_copies[t].wait()

        @pl.loop(0, TILE // rows_ln)
        def _(b):
            rows = pl.ds(pl.multiple_of(t * TILE + b * rows_ln, rows_ln), rows_ln)
            h = hid[rows, :].astype(F32)
            mu = jnp.mean(h, axis=-1, keepdims=True)
            cen = h - mu
            rs = lax.rsqrt(jnp.mean(cen * cen, axis=-1, keepdims=True) + LN_EPS)
            x_own[rows, :] = (cen * rs * gain[...] + bias[...]).astype(BF16)
            mu_s[rows, :] = jnp.broadcast_to(mu, (rows_ln, LANES))
            rs_s[rows, :] = jnp.broadcast_to(rs, (rows_ln, LANES))

    x_out = pltpu.make_async_copy(x_own, x_h.at[me], loc_sem.at[1])
    x_out.start()
    e_own.wait()

    def z_store(st, v):
        return pltpu.make_async_copy(zb.at[pl.ds(st * tiles, tiles)], z_h.at[v], z_sem.at[st])

    def stats(slot, q, st):
        e_piece = e_all[slot, pl.ds(pl.multiple_of(q * PIECE, PIECE), PIECE), :]
        half = tokens // 2
        for h in range(2):
            z = matmul_t(x_own[h * half:(h + 1) * half, :], e_piece)
            for b in range(half // TILE):
                zb[st * tiles + h * (half // TILE) + b] = z[b * TILE:(b + 1) * TILE, :]
        per = TILE // LANES
        for b in range(blocks):
            rows = slice(b * LANES, (b + 1) * LANES)
            z = zb[st * tiles + b // per, (b % per) * LANES:(b % per + 1) * LANES, :]
            z0, z1 = z[:, :LANES], z[:, LANES:]
            old = max_s[rows, :]
            new = jnp.maximum(old, jnp.maximum(z0, z1))
            sum_s[rows, :] = sum_s[rows, :] * jnp.exp(old - new) + jnp.exp(z0 - new) + jnp.exp(z1 - new)
            max_s[rows, :] = new

    @pl.loop(0, 2 * e_parts)
    def _(i):
        lane, q = i // e_parts, i % e_parts
        slot = me + lane * (1 - 2 * core)

        @pl.when(i == e_parts)
        def _():
            e_swap.wait_recv()

        @pl.when(i >= 2)
        def _():
            z_store(i % 2, 0).wait()
        stats(slot, q, i % 2)
        z_store(i % 2, slot * e_parts + q).start()

    x_out.wait()
    x_swap = remote(x_h.at[me], x_h.at[me], x_pair.at[0], x_pair.at[1], partner)
    x_swap.start()

    @pl.loop(0, e_rounds)
    def _(k):
        for d in range(2):
            e_wait(k, d)
        for d in range(2):
            e_relay(k, d, 0).start()

        @pl.when(k < e_parts // 2)
        def _():
            for d in range(2):
                e_ring(k + e_parts, d).start()

        @pl.when(k == e_parts // 2)
        def _():
            for j in range(2):
                for d in range(2):
                    x_ring(j, d).start()

        @pl.loop(0, 4)
        def _(i):
            lane, d = i // 2, i % 2

            @pl.when(i == 2)
            def _():
                for dd in range(2):
                    e_relay(k, dd, 1).wait_recv()
            slot, q = arrival(k, d, e_parts, lane)
            z_store(i % 2, 0).wait()
            stats(slot, q, i % 2)
            z_store(i % 2, slot * e_parts + q).start()

    for b in range(blocks):
        rows = slice(b * LANES, (b + 1) * LANES)
        part = max_s[rows, :]
        top = jnp.max(part, axis=-1, keepdims=True)
        tot = jnp.sum(sum_s[rows, :] * jnp.exp(part - top), axis=-1, keepdims=True)
        lse = jnp.broadcast_to(top + jnp.log(tot), (LANES, LANES))
        max_s[rows, :] = lse
        ls_all[me, b:b + 1, :] = jnp.transpose(lse)[0:1, :]
        sum_s[rows, :] = jnp.zeros((LANES, LANES), F32)
    for cp in mk_copies + tg_copies:
        cp.wait_recv()
    count = jnp.sum(jnp.sum(jnp.sum(mk_all[...].astype(F32), axis=0), axis=0, keepdims=True), axis=1, keepdims=True)
    inv_s[...] = jnp.broadcast_to(1.0 / count, inv_s.shape)
    for st in range(2):
        z_store(st, 0).wait()
    ls_copies = to_all(ls_all.at[me], ls_all.at[me], ls_sem)
    for cp in ls_copies:
        cp.start()

    chunks = n * shard // TILE
    halves = TILE // PIECE
    depth = 3

    def z_load(u, h):
        return pltpu.make_async_copy(z_h.at[(u % chunks) * halves + h, u // chunks], zb.at[(u % 4) * halves + h], zl_sem.at[u % 4, h])

    for u in range(depth):
        for h in range(halves):
            z_load(u, h).start()
    for j in range(2, x_parts):
        for d in range(2):
            x_ring(j, d).start()

    lane_ids = lax.broadcasted_iota(jnp.int32, (1, LANES), 1)

    def make_dz(t, vc, out):
        u = t * chunks + vc
        for h in range(halves):
            z_load(u, h).wait()

        @pl.when(u + depth < tiles * chunks)
        def _():
            for h in range(halves):
                z_load(u + depth, h).start()

        def work():
            slot = (u % 4) * halves
            for b in range(TILE // LANES):
                rows = slice(b * LANES, (b + 1) * LANES)
                tok = pl.ds(pl.multiple_of(t * TILE + b * LANES, LANES), LANES)
                lse, tc, wc = max_s[tok, :], tcol[rows, :], wcol[rows, :]
                found = sum_s[tok, :]
                for g in range(TILE // LANES):
                    lo = (g * LANES) % PIECE
                    z = zb[slot + g * LANES // PIECE, rows, lo:lo + LANES]
                    hit = tc == (lane_ids + (vc * TILE + g * LANES)).astype(F32)
                    p = jnp.exp(z - lse)
                    out[rows, g * LANES:(g + 1) * LANES] = (jnp.where(hit, p - 1.0, p) * wc).astype(BF16)
                    found = found + jnp.where(hit, z, 0.0)
                sum_s[tok, :] = found
        return work

    @pl.loop(0, tiles)
    def _(t):
        for b in range(TILE // LANES):
            row = pl.ds(t * (TILE // LANES) + b, 1)
            rows = slice(b * LANES, (b + 1) * LANES)
            tcol[rows, :] = to_col(tg_all[me, row, :].astype(F32))
            wcol[rows, :] = to_col(mk_all[me, row, :].astype(F32) * inv_s[0:1, :])
        dx_acc[...] = jnp.zeros_like(dx_acc)
        da = dz_a.at[pl.ds(0, TILE), :]
        db = dz_b.at[pl.ds(0, TILE), :]
        make_dz(t, 0, da)()

        @pl.loop(0, n - 1)
        def _(v):
            work = make_dz(t, 2 * v + 1, db)
            dx_acc[...] += matmul(da[...], e_all[v, 0:TILE, :])
            work()
            work = make_dz(t, 2 * v + 2, da)
            dx_acc[...] += matmul(db[...], e_all[v, TILE:2 * TILE, :])
            work()
        work = make_dz(t, chunks - 1, db)
        dx_acc[...] += matmul(da[...], e_all[n - 1, 0:TILE, :])
        work()
        dx_acc[...] += matmul(db[...], e_all[n - 1, TILE:2 * TILE, :])

        rows_bw = 32

        @pl.loop(0, TILE // rows_bw)
        def _(b):
            loc = pl.ds(pl.multiple_of(b * rows_bw, rows_bw), rows_bw)
            rows = pl.ds(pl.multiple_of(t * TILE + b * rows_bw, rows_bw), rows_bw)
            dx = dx_acc[loc, :]
            rs = widen(rs_s[rows, :], dim)
            xh = (hid[rows, :].astype(F32) - widen(mu_s[rows, :], dim)) * rs
            dxx = dx * xh

            @pl.when(t + b == 0)
            def _():
                gb[...] = jnp.zeros_like(gb)
            gb[0:8, :] += jnp.sum(dxx.reshape(rows_bw // 8, 8, dim), axis=0)
            gb[8:16, :] += jnp.sum(dx.reshape(rows_bw // 8, 8, dim), axis=0)
            g = dx * gain[...]
            c1 = jnp.mean(g, axis=-1, keepdims=True)
            c2 = jnp.mean(g * xh, axis=-1, keepdims=True)
            hid[rows, :] = (rs * (g - c1 - xh * c2)).astype(BF16)
        for b in range(TILE // LANES):
            row = pl.ds(t * (TILE // LANES) + b, 1)
            tok = pl.ds(pl.multiple_of(t * TILE + b * LANES, LANES), LANES)
            t_row = to_row(jnp.sum(sum_s[tok, :], axis=-1, keepdims=True))
            loss_o[row, :] = (ls_all[me, row, :] - t_row) * mk_all[me, row, :].astype(F32)
        out_rows = pl.ds(pl.multiple_of(t * TILE, TILE), TILE)
        pltpu.make_async_copy(hid.at[out_rows, :], dh_o.at[out_rows, :], dh_sem.at[t]).start()

    sm_all[me] = jnp.zeros(sm_all.shape[1:], F32)
    sm_all[me, 0:1, :] = jnp.sum(gb[0:8, :], axis=0, keepdims=True)
    sm_all[me, 1:2, :] = jnp.sum(gb[8:16, :], axis=0, keepdims=True)
    loss_sum = jnp.sum(jnp.sum(loss_o[...], axis=0, keepdims=True), axis=1, keepdims=True)
    sm_all[me, 2:3, :] = jnp.broadcast_to(loss_sum, (1, dim))

    de_acc[...] = jnp.zeros_like(de_acc)
    dz_b[...] = jnp.zeros_like(dz_b)
    xbuf[1, 1] = jnp.zeros(xbuf.shape[2:], BF16)
    for cp in ls_copies:
        cp.wait_recv()
    sm_copies = to_all(sm_all.at[me], sm_all.at[me], sm_sem)
    for cp in sm_copies:
        cp.start()
    x_swap.wait_recv()
    lead = x_parts // 2
    pairs = lead + x_rounds
    early = x_parts // 2

    def source(p, lane, d):
        far = (p + x_rounds) // pairs
        k = p - lead * far
        off = (2 * d - 1) * far * (1 + k // x_parts)
        side = core + lane * (1 - 2 * core)
        slot = 2 * ((chip + off + chips) % chips) + side
        q = far * ((k + d * (x_parts // 2)) % x_parts) + (1 - far) * (2 * p + d)
        return slot, q

    def x_load(p, lane, d):
        slot, q = source(p, lane, d)
        return pltpu.make_async_copy(piece(x_h, slot, q), xbuf.at[p % 2, lane, pl.ds(d * PIECE, PIECE), :], xl_sem.at[lane, d])

    base = me * shard

    def vocab_step(p, lane, dz_out, dz_in, xd):
        zt[...] = matmul_t(e_all[me], xbuf[p % 2, lane])
        de_acc[...] += matmul(dz_in[...], xd[...])
        cols = []
        for d in range(2):
            slot, q = source(p, lane, d)
            for r in range(PIECE // LANES):
                row = pl.ds(q * (PIECE // LANES) + r, 1)
                cols.append((ls_all[slot, row, :], tg_all[slot, row, :] - base, mk_all[slot, row, :].astype(F32) * inv_s[0:1, :]))
        ids = lax.broadcasted_iota(jnp.int32, (LANES, LANES), 0)
        for b in range(shard // LANES):
            rows = slice(b * LANES, (b + 1) * LANES)
            for g, (lse, tg, sc) in enumerate(cols):
                lanes = slice(g * LANES, (g + 1) * LANES)
                pr = jnp.exp(zt[rows, lanes] - lse)
                hit = ids == tg - b * LANES
                dz_out[rows, lanes] = (jnp.where(hit, pr - 1.0, pr) * sc).astype(BF16)

    for d in range(2):
        x_load(0, 0, d).start()

    @pl.loop(0, pairs)
    def _(p):
        @pl.when(p == 1)
        def _():
            for k in range(early):
                for d in range(2):
                    x_wait(k, d)
                for d in range(2):
                    x_ring(k + x_parts, d).start()
                for d in range(2):
                    x_relay(k, d, 0).start()

        @pl.when(p >= lead)
        def _():
            for d in range(2):
                x_relay(p - lead, d, 1).wait_recv()
        for d in range(2):
            x_load(p, 1, d).start()
        for d in range(2):
            x_load(p, 0, d).wait()
        vocab_step(p, 0, dz_a, dz_b, xbuf.at[1 - p % 2, 1])

        @pl.when(p + 1 >= lead + early)
        def _():
            @pl.when(p + 1 < pairs)
            def _():
                for d in range(2):
                    x_wait(p + 1 - lead, d)
                for d in range(2):
                    x_relay(p + 1 - lead, d, 0).start()

        @pl.when(p + 1 < pairs)
        def _():
            for d in range(2):
                x_load(p + 1, 0, d).start()
        for d in range(2):
            x_load(p, 1, d).wait()
        vocab_step(p, 1, dz_b, dz_a, xbuf.at[p % 2, 0])

    de_acc[...] += matmul(dz_b[...], xbuf[(pairs - 1) % 2, 1])
    de_out = pltpu.make_async_copy(de_acc, de_o, loc_sem.at[0])
    de_out.start()

    for cp in sm_copies:
        cp.wait_recv()
    total = sm_all[0]
    for r in range(1, n):
        total = total + sm_all[r]
    dg_o[...] = total[0:1, :]
    db_o[...] = total[1:2, :]
    mean_o[...] = total[2:3, 0:LANES] * inv_s[0:1, :]

    for cp in tg_copies + mk_copies + ls_copies + sm_copies:
        cp.wait_send()
    e_swap.wait_send()
    x_swap.wait_send()

    @pl.loop(0, e_rounds)
    def _(j):
        for d in range(2):
            e_ring(j, d).wait_send()
            e_relay(j, d, 0).wait_send()

    @pl.loop(0, x_rounds)
    def _(j):
        for d in range(2):
            x_ring(j, d).wait_send()
            x_relay(j, d, 0).wait_send()

    for t in range(tiles):
        rows = pl.ds(t * TILE, TILE)
        pltpu.make_async_copy(hid.at[rows, :], dh_o.at[rows, :], dh_sem.at[t]).wait()
    de_out.wait()


def solution(mesh):
    n = mesh.shape['tp']

    def body(hidden, ln_gain, ln_bias, embed, targets, loss_mask):
        tokens, dim = hidden.shape
        shard = embed.shape[0]
        blocks = tokens // LANES
        e_rounds = shard // PIECE * 3 // 2
        x_rounds = tokens // PIECE * 3 // 2
        tiles = tokens // TILE
        anywhere = pl.BlockSpec(memory_space=pl.ANY)
        vmem = pl.BlockSpec(memory_space=pltpu.VMEM)
        dma = pltpu.SemaphoreType.DMA
        sds = jax.ShapeDtypeStruct
        outs = pl.pallas_call(
            functools.partial(kernel, n),
            out_shape=(
                sds((blocks, LANES), F32), sds((1, LANES), F32), sds((tokens, dim), BF16), sds((shard, dim), F32),
                sds((1, dim), F32), sds((1, dim), F32),
                sds((n * shard // PIECE, tiles, TILE, PIECE), F32), sds((n, tokens, dim), BF16),
            ),
            in_specs=[anywhere, vmem, vmem, anywhere, vmem, vmem],
            out_specs=(vmem, vmem, anywhere, anywhere, vmem, vmem, anywhere, anywhere),
            scratch_shapes=[
                pltpu.VMEM((n, shard, dim), BF16), pltpu.VMEM((tokens, dim), BF16), pltpu.VMEM((tokens, dim), BF16),
                pltpu.VMEM((shard, dim), F32), pltpu.VMEM((tokens, LANES), F32), pltpu.VMEM((tokens, LANES), F32),
                pltpu.VMEM((tokens, LANES), F32), pltpu.VMEM((tokens, LANES), F32),
                pltpu.VMEM((2, 2, TILE, dim), BF16), pltpu.VMEM((shard, TILE), BF16), pltpu.VMEM((shard, TILE), BF16),
                pltpu.VMEM((8, TILE, PIECE), F32), pltpu.VMEM((TILE, dim), F32), pltpu.VMEM((shard, TILE), F32),
                pltpu.VMEM((TILE, LANES), F32), pltpu.VMEM((TILE, LANES), F32),
                pltpu.VMEM((n, blocks, LANES), jnp.int32), pltpu.VMEM((n, blocks, LANES), jnp.int32),
                pltpu.VMEM((n, blocks, LANES), F32), pltpu.VMEM((n, 8, dim), F32), pltpu.VMEM((16, dim), F32),
                pltpu.VMEM((8, LANES), F32),
                dma((2, e_rounds)), dma((2, e_rounds)), dma((2, e_rounds)), dma((2, e_rounds)), dma((2,)),
                dma((2, x_rounds)), dma((2, x_rounds)), dma((2, x_rounds)), dma((2, x_rounds)), dma((2,)),
                dma((2, n)), dma((2, n)), dma((2, n)), dma((2, n)),
                dma((tiles,)), dma((2,)), dma((2,)), dma((4, 2)), dma((2, 2)), dma((tiles,)),
            ],
            compiler_params=pltpu.CompilerParams(collective_id=0, has_side_effects=True, vmem_limit_bytes=60 * 1024 * 1024),
        )(hidden, ln_gain.reshape(1, dim), ln_bias.reshape(1, dim), embed, targets.reshape(blocks, LANES), loss_mask.reshape(blocks, LANES))
        loss, mean, d_hidden, d_embed, d_gain, d_bias = outs[:6]
        return loss.reshape(tokens), mean[0, :1], d_hidden, d_embed, d_gain.reshape(dim), d_bias.reshape(dim)

    rows = P(('dp', 'tp'))
    mat = P(('dp', 'tp'), None)
    return jax.shard_map(body, mesh=mesh, in_specs=(mat, P(), P(), P('tp', None), rows, rows), out_specs=(rows, P('dp'), mat, mat, P('dp'), P('dp')), check_vma=False)
```

time: 425 us -> 265 us (0.62)
  Pallas kernels: 0 us -> 253 us
  waiting for transfers between devices: 156 us -> 0 us
  matrix products: 139 us -> 0 us
  other arithmetic: 75.4 us -> 0 us
  blocking collectives: 35.9 us -> 0 us
  between operations: 16.6 us -> 2.48 us
  local copies, waits for them, and re-layouts: 1.77 us -> 9.33 us
    pallas_call x0 -> x1, Pallas kernels: none -> 253 us  [body(): pl.pallas_call(functools.partial(kernel, n), out_shape=(sds((blocks, LANE...]
    dot_general x3 -> x0, matrix products: 139 us -> none  [the longest x1 47.1 us: body(): jnp.einsum('sd,vd->sv', normed, table, preferred_element_type=jnp.float32)]
    reduce_scatter x1 -> x0, waiting for transfers between devices: 88.9 us -> none  [body(): lax.psum_scatter(d_embed_part, 'tp', scatter_dimension=0, tiled=True)]
    all_gather x1 -> x0, waiting for transfers between devices: 66.7 us -> none  [body(): table = lax.all_gather(embed, 'tp', tiled=True)]
    convert_element_type x2 -> x0, other arithmetic: 40.7 us -> none  [the longest x1 33.5 us: body(): ((jnp.exp(logits - log_norm[:, None]) - onehot.astype(jnp.float32)) * (we...]
    psum x2 -> x0, blocking collectives: 35.9 us -> none  [the longest x1 21.5 us: body(): sums = lax.psum(sums, 'tp')]
    reduce_sum x5 -> x0, other arithmetic: 34.7 us -> none  [the longest x1 25.8 us: body(): t_logit = jnp.sum(jnp.where(onehot, logits, 0.0), axis=-1)]
    unnamed x8 -> x11, local copies, waits for them, and re-layouts: 0.02 us -> 9.33 us
  transfers between devices with their start and end apart: 2 -> 0, of which waited for: 2 -> 0; matrix products, arithmetic and copies ran while one was open for 15% -> 0% of each run, Pallas kernels for 0% -> 0%
where the time goes in v2:
time: 265 us
  Pallas kernels  253 us (95%)
  local copies, waits for them, and re-layouts  9.33 us (4%)
    pallas_call x1, Pallas kernels, body(): pl.pallas_call(functools.partial(kernel, n), out_shape=(sds((blocks, LANE...  253 us
    unnamed x11, local copies, waits for them, and re-layouts  9.33 us

profile of v2, /device:TPU:81, one launch (start us, length us, event | category | flops | bytes accessed | tf_op | source)
XLA Modules:
  0.0 264.6 jit_solution(2229464588333662881)
XLA Ops:
  0.6 252.7 %shard_map.109 = (f32[16,128]{1,0:T(8,128)}, f32[1,128]{1,0:T(1,128)}, bf16[2048,1024]{1,0:T(8,128)(2,1)}, f32[1024,1024]{1,0:T(8,128)}, f32[1,1024]{1,0:T(1,128...) custom-call(bf16[2048,1024]{1,0:T(8,128)(2,1)} %hidden.1, f32[1,1024]{1,0:T(1,128)} %bitcast.12, ...), custom_call_target="tpu_custom_call" | custom-call | tf_op jit(solution)/shard_map/pallas_call | solution.py:484
  253.4 1.3 copy.18
  255.4 0.0 copy-start
  255.4 4.8 %copy.20 = bf16[2048,1024]{1,0:T(8,128)(2,1)} copy(bf16[2048,1024]{1,0:T(8,128)(2,1)} %get-tuple-element.26) | data formatting | bytes 8388608
  260.2 0.0 copy-done
  260.2 0.0 copy-start.2
  260.2 0.0 copy-start.1
  260.2 2.0 copy.21
  262.2 0.0 copy-done.2
  262.2 0.6 copy.22
  262.8 0.0 copy-done.1
  262.8 0.6 copy.23
Async XLA Ops:
  255.4 4.8 %copy-start = (f32[1024,1024]{1,0:T(8,128)S(1)}, f32[1024,1024]{1,0:T(8,128)}, u32[]{:S(2)}) copy-start(f32[1024,1024]{1,0:T(8,128)} %get-tuple-element.27) | copy-start | bytes 12582916
  260.2 2.0 copy-start.2
  260.2 2.6 copy-start.1

commit v3 on v2

--- a/solution.py
+++ b/solution.py
@@ -37,11 +37,11 @@
 
 
 def kernel(n, hidden, gain, bias, embed, tgt, msk,
-           loss_o, mean_o, dh_o, de_o, dg_o, db_o, z_h, x_h,
-           e_all, x_own, hid, de_acc, max_s, sum_s, mu_s, rs_s, xbuf, dz_a, dz_b, zb, dx_acc, zt,
+           loss_o, mean_o, dh_o, de_o, dg_o, db_o, z_h, x_h, zt_h,
+           e_all, x_own, hid, de_acc, max_s, sum_s, mu_s, rs_s, xbuf, dz_a, dz_b, zb, dx_0, dx_1, dh_0, dh_1, zt_0, zt_1,
            tcol, wcol, tg_all, mk_all, ls_all, sm_all, gb, inv_s,
            e_send, e_recv, ep_send, ep_recv, e_pair, x_send, x_recv, xp_send, xp_recv, x_pair,
-           tg_sem, mk_sem, ls_sem, sm_sem, hid_sem, loc_sem, z_sem, zl_sem, xl_sem, dh_sem):
+           tg_sem, mk_sem, ls_sem, sm_sem, hid_sem, loc_sem, z_sem, zl_sem, xl_sem, dh_sem, zt_sem, xi_sem):
     tokens, dim = hid.shape
     shard = embed.shape[0]
     chips = n // 2
@@ -54,6 +54,7 @@
     partner = 2 * chip + 1 - core
     right, left = (me + 2) % n, (me + n - 2) % n
     ring_dev = (right, left)
+    dxs, dhs, zts = (dx_0, dx_1), (dh_0, dh_1), (zt_0, zt_1)
 
     def remote(src, dst, ssem, rsem, dev):
         return pltpu.make_async_remote_copy(src_ref=src, dst_ref=dst, send_sem=ssem, recv_sem=rsem,
@@ -151,6 +152,15 @@
     x_out = pltpu.make_async_copy(x_own, x_h.at[me], loc_sem.at[1])
     x_out.start()
     e_own.wait()
+
+    for cp in mk_copies + tg_copies:
+        cp.wait_recv()
+    count = jnp.sum(jnp.sum(jnp.sum(mk_all[...].astype(F32), axis=0), axis=0, keepdims=True), axis=1, keepdims=True)
+    inv_s[...] = jnp.broadcast_to(1.0 / count, inv_s.shape)
+    for b in range(blocks):
+        rows = slice(b * LANES, (b + 1) * LANES)
+        tcol[rows, :] = to_col(tgt[b:b + 1, :].astype(F32))
+        wcol[rows, :] = to_col(msk[b:b + 1, :].astype(F32) * inv_s[0:1, :])
 
     def z_store(st, v):
         return pltpu.make_async_copy(zb.at[pl.ds(st * tiles, tiles)], z_h.at[v], z_sem.at[st])
@@ -191,6 +201,16 @@
     x_swap = remote(x_h.at[me], x_h.at[me], x_pair.at[0], x_pair.at[1], partner)
     x_swap.start()
 
+    def zt_store(s, lane, t):
+        return pltpu.make_async_copy(zts[s], zt_h.at[lane, t], zt_sem.at[s])
+
+    def zt_load(lane, t):
+        return pltpu.make_async_copy(zt_h.at[lane, t], zts[lane], zt_sem.at[lane])
+
+    def near_load(s, lane, t):
+        slot = me + lane * (1 - 2 * core)
+        return pltpu.make_async_copy(x_h.at[slot, pl.ds(pl.multiple_of(t * TILE, TILE), TILE), :], xbuf.at[s, 0], xi_sem.at[s])
+
     @pl.loop(0, e_rounds)
     def _(k):
         for d in range(2):
@@ -221,6 +241,26 @@
             z_store(i % 2, 0).wait()
             stats(slot, q, i % 2)
             z_store(i % 2, slot * e_parts + q).start()
+
+        @pl.when(k == 1 + tiles // 2)
+        def _():
+            x_swap.wait_recv()
+
+        @pl.when(k >= 1)
+        def _():
+            @pl.when(k <= tiles)
+            def _():
+                pos = 2 * (k - 1)
+                for s in range(2):
+                    near_load(s, (pos + s) // tiles, (pos + s) % tiles).start()
+                for s in range(2):
+                    near_load(s, 0, 0).wait()
+
+                    @pl.when(k > 1)
+                    def _():
+                        zt_store(s, 0, 0).wait()
+                    zts[s][...] = matmul_t(e_all[me], xbuf[s, 0])
+                    zt_store(s, (pos + s) // tiles, (pos + s) % tiles).start()
 
     for b in range(blocks):
         rows = slice(b * LANES, (b + 1) * LANES)
@@ -231,111 +271,118 @@
         max_s[rows, :] = lse
         ls_all[me, b:b + 1, :] = jnp.transpose(lse)[0:1, :]
         sum_s[rows, :] = jnp.zeros((LANES, LANES), F32)
-    for cp in mk_copies + tg_copies:
-        cp.wait_recv()
-    count = jnp.sum(jnp.sum(jnp.sum(mk_all[...].astype(F32), axis=0), axis=0, keepdims=True), axis=1, keepdims=True)
-    inv_s[...] = jnp.broadcast_to(1.0 / count, inv_s.shape)
     for st in range(2):
         z_store(st, 0).wait()
+        zt_store(st, 0, 0).wait()
     ls_copies = to_all(ls_all.at[me], ls_all.at[me], ls_sem)
     for cp in ls_copies:
         cp.start()
 
-    chunks = n * shard // TILE
-    halves = TILE // PIECE
-    depth = 3
-
-    def z_load(u, h):
-        return pltpu.make_async_copy(z_h.at[(u % chunks) * halves + h, u // chunks], zb.at[(u % 4) * halves + h], zl_sem.at[u % 4, h])
-
-    for u in range(depth):
-        for h in range(halves):
-            z_load(u, h).start()
+    steps = tiles * n
+
+    def z_load(u):
+        return pltpu.make_async_copy(z_h.at[pl.ds((u % n) * e_parts, e_parts), (u // n) % tiles], zb.at[pl.ds((u % 2) * e_parts, e_parts)], zl_sem.at[u % 2])
+
+    for u in range(2):
+        z_load(u).start()
     for j in range(2, x_parts):
         for d in range(2):
             x_ring(j, d).start()
 
     lane_ids = lax.broadcasted_iota(jnp.int32, (1, LANES), 1)
 
-    def make_dz(t, vc, out):
-        u = t * chunks + vc
-        for h in range(halves):
-            z_load(u, h).wait()
-
-        @pl.when(u + depth < tiles * chunks)
-        def _():
-            for h in range(halves):
-                z_load(u + depth, h).start()
-
-        def work():
-            slot = (u % 4) * halves
-            for b in range(TILE // LANES):
-                rows = slice(b * LANES, (b + 1) * LANES)
-                tok = pl.ds(pl.multiple_of(t * TILE + b * LANES, LANES), LANES)
-                lse, tc, wc = max_s[tok, :], tcol[rows, :], wcol[rows, :]
-                found = sum_s[tok, :]
-                for g in range(TILE // LANES):
-                    lo = (g * LANES) % PIECE
-                    z = zb[slot + g * LANES // PIECE, rows, lo:lo + LANES]
-                    hit = tc == (lane_ids + (vc * TILE + g * LANES)).astype(F32)
-                    p = jnp.exp(z - lse)
-                    out[rows, g * LANES:(g + 1) * LANES] = (jnp.where(hit, p - 1.0, p) * wc).astype(BF16)
-                    found = found + jnp.where(hit, z, 0.0)
-                sum_s[tok, :] = found
-        return work
-
-    @pl.loop(0, tiles)
-    def _(t):
+    def make_dz(u, out):
+        t, v = (u // n) % tiles, u % n
+        slot = (u % 2) * e_parts
         for b in range(TILE // LANES):
-            row = pl.ds(t * (TILE // LANES) + b, 1)
             rows = slice(b * LANES, (b + 1) * LANES)
-            tcol[rows, :] = to_col(tg_all[me, row, :].astype(F32))
-            wcol[rows, :] = to_col(mk_all[me, row, :].astype(F32) * inv_s[0:1, :])
-        dx_acc[...] = jnp.zeros_like(dx_acc)
-        da = dz_a.at[pl.ds(0, TILE), :]
-        db = dz_b.at[pl.ds(0, TILE), :]
-        make_dz(t, 0, da)()
-
-        @pl.loop(0, n - 1)
-        def _(v):
-            work = make_dz(t, 2 * v + 1, db)
-            dx_acc[...] += matmul(da[...], e_all[v, 0:TILE, :])
-            work()
-            work = make_dz(t, 2 * v + 2, da)
-            dx_acc[...] += matmul(db[...], e_all[v, TILE:2 * TILE, :])
-            work()
-        work = make_dz(t, chunks - 1, db)
-        dx_acc[...] += matmul(da[...], e_all[n - 1, 0:TILE, :])
-        work()
-        dx_acc[...] += matmul(db[...], e_all[n - 1, TILE:2 * TILE, :])
-
-        rows_bw = 32
-
-        @pl.loop(0, TILE // rows_bw)
-        def _(b):
-            loc = pl.ds(pl.multiple_of(b * rows_bw, rows_bw), rows_bw)
-            rows = pl.ds(pl.multiple_of(t * TILE + b * rows_bw, rows_bw), rows_bw)
-            dx = dx_acc[loc, :]
+            tok = pl.ds(pl.multiple_of(t * TILE + b * LANES, LANES), LANES)
+            lse, tc, wc = max_s[tok, :], tcol[tok, :], wcol[tok, :]
+            found = sum_s[tok, :]
+            for g in range(shard // LANES):
+                lo = (g * LANES) % PIECE
+                z = zb[slot + g * LANES // PIECE, rows, lo:lo + LANES]
+                hit = tc == (lane_ids + (v * shard + g * LANES)).astype(F32)
+                p = jnp.exp(z - lse)
+                top, at = g * LANES // TILE * TILE + b * LANES, (g * LANES) % TILE
+                out[top:top + LANES, at:at + LANES] = (jnp.where(hit, p - 1.0, p) * wc).astype(BF16)
+                found = found + jnp.where(hit, z, 0.0)
+            sum_s[tok, :] = found
+
+    def norm_back(t, at, count_rows, dx_ref, dh_ref):
+        step = 32
+        for b in range(count_rows // step):
+            loc = pl.ds(pl.multiple_of(at + b * step, step), step)
+            rows = pl.ds(pl.multiple_of(t * TILE + at + b * step, step), step)
+            dx = dx_ref[loc, :]
+            dx_ref[loc, :] = jnp.zeros_like(dx)
             rs = widen(rs_s[rows, :], dim)
             xh = (hid[rows, :].astype(F32) - widen(mu_s[rows, :], dim)) * rs
-            dxx = dx * xh
-
-            @pl.when(t + b == 0)
-            def _():
-                gb[...] = jnp.zeros_like(gb)
-            gb[0:8, :] += jnp.sum(dxx.reshape(rows_bw // 8, 8, dim), axis=0)
-            gb[8:16, :] += jnp.sum(dx.reshape(rows_bw // 8, 8, dim), axis=0)
+            gb[0:8, :] += jnp.sum((dx * xh).reshape(step // 8, 8, dim), axis=0)
+            gb[8:16, :] += jnp.sum(dx.reshape(step // 8, 8, dim), axis=0)
             g = dx * gain[...]
             c1 = jnp.mean(g, axis=-1, keepdims=True)
             c2 = jnp.mean(g * xh, axis=-1, keepdims=True)
-            hid[rows, :] = (rs * (g - c1 - xh * c2)).astype(BF16)
-        for b in range(TILE // LANES):
-            row = pl.ds(t * (TILE // LANES) + b, 1)
-            tok = pl.ds(pl.multiple_of(t * TILE + b * LANES, LANES), LANES)
-            t_row = to_row(jnp.sum(sum_s[tok, :], axis=-1, keepdims=True))
-            loss_o[row, :] = (ls_all[me, row, :] - t_row) * mk_all[me, row, :].astype(F32)
-        out_rows = pl.ds(pl.multiple_of(t * TILE, TILE), TILE)
-        pltpu.make_async_copy(hid.at[out_rows, :], dh_o.at[out_rows, :], dh_sem.at[t]).start()
+            dh_ref[loc, :] = (rs * (g - c1 - xh * c2)).astype(BF16)
+
+    def dh_out(t, s):
+        return pltpu.make_async_copy(dhs[s], dh_o.at[pl.ds(pl.multiple_of(t * TILE, TILE), TILE), :], dh_sem.at[s])
+
+    gb[...] = jnp.zeros_like(gb)
+    for s in range(2):
+        dxs[s][...] = jnp.zeros_like(dxs[s])
+    z_load(0).wait()
+    make_dz(0, dz_a)
+    z_load(2).start()
+
+    @pl.loop(0, tiles // 2)
+    def _(tt):
+        for s in range(2):
+            t = 2 * tt + s
+            prev = (t + tiles - 1) % tiles
+            other = 1 - s
+
+            @pl.when(t >= 3)
+            def _():
+                dh_out(0, other).wait()
+
+            @pl.loop(0, n // 2)
+            def _(w):
+                for half, (now, later) in enumerate(((dz_a, dz_b), (dz_b, dz_a))):
+                    v = 2 * w + half
+                    u = t * n + v + 1
+                    z_load(u).wait()
+                    dxs[s][...] += matmul(now[0:TILE, :], e_all[v, 0:TILE, :]) + matmul(now[TILE:2 * TILE, :], e_all[v, TILE:2 * TILE, :])
+                    make_dz(u, later)
+                    norm_back(prev, v * (TILE // n), TILE // n, dxs[other], dhs[other])
+
+                    @pl.when(u + 2 <= steps)
+                    def _():
+                        z_load(u + 2).start()
+
+            @pl.when(t >= 1)
+            def _():
+                dh_out(prev, other).start()
+            for b in range(TILE // LANES):
+                row = pl.ds(t * (TILE // LANES) + b, 1)
+                tok = pl.ds(pl.multiple_of(t * TILE + b * LANES, LANES), LANES)
+                t_row = to_row(jnp.sum(sum_s[tok, :], axis=-1, keepdims=True))
+                loss_o[row, :] = (ls_all[me, row, :] - t_row) * msk[row, :].astype(F32)
+
+            for d in range(2):
+                x_wait(t, d)
+            for d in range(2):
+                x_ring(t + x_parts, d).start()
+            for d in range(2):
+                x_relay(t, d, 0).start()
+
+    last = (tiles - 1) % 2
+    dh_out(0, last).wait()
+
+    @pl.loop(0, n)
+    def _(b):
+        norm_back(tiles - 1, b * (TILE // n), TILE // n, dxs[last], dhs[last])
+    dh_out(tiles - 1, last).start()
 
     sm_all[me] = jnp.zeros(sm_all.shape[1:], F32)
     sm_all[me, 0:1, :] = jnp.sum(gb[0:8, :], axis=0, keepdims=True)
@@ -351,7 +398,6 @@
     sm_copies = to_all(sm_all.at[me], sm_all.at[me], sm_sem)
     for cp in sm_copies:
         cp.start()
-    x_swap.wait_recv()
     lead = x_parts // 2
     pairs = lead + x_rounds
     early = x_parts // 2
@@ -371,8 +417,10 @@
 
     base = me * shard
 
-    def vocab_step(p, lane, dz_out, dz_in, xd):
-        zt[...] = matmul_t(e_all[me], xbuf[p % 2, lane])
+    def vocab_step(p, lane, dz_out, dz_in, xd, fresh):
+        zt = zts[lane]
+        if fresh:
+            zt[...] = matmul_t(e_all[me], xbuf[p % 2, lane])
         de_acc[...] += matmul(dz_in[...], xd[...])
         cols = []
         for d in range(2):
@@ -391,45 +439,55 @@
 
     for d in range(2):
         x_load(0, 0, d).start()
-
-    @pl.loop(0, pairs)
+    for lane in range(2):
+        zt_load(lane, 0).start()
+
+    @pl.loop(0, lead)
     def _(p):
-        @pl.when(p == 1)
-        def _():
-            for k in range(early):
-                for d in range(2):
-                    x_wait(k, d)
-                for d in range(2):
-                    x_ring(k + x_parts, d).start()
-                for d in range(2):
-                    x_relay(k, d, 0).start()
-
-        @pl.when(p >= lead)
-        def _():
-            for d in range(2):
-                x_relay(p - lead, d, 1).wait_recv()
         for d in range(2):
             x_load(p, 1, d).start()
         for d in range(2):
             x_load(p, 0, d).wait()
-        vocab_step(p, 0, dz_a, dz_b, xbuf.at[1 - p % 2, 1])
-
-        @pl.when(p + 1 >= lead + early)
-        def _():
-            @pl.when(p + 1 < pairs)
+        zt_load(0, 0).wait()
+        vocab_step(p, 0, dz_a, dz_b, xbuf.at[1 - p % 2, 1], False)
+
+        @pl.when(p + 1 < lead)
+        def _():
+            zt_load(0, p + 1).start()
+        for d in range(2):
+            x_load(p + 1, 0, d).start()
+        for d in range(2):
+            x_load(p, 1, d).wait()
+        zt_load(1, 0).wait()
+        vocab_step(p, 1, dz_b, dz_a, xbuf.at[p % 2, 0], False)
+
+        @pl.when(p + 1 < lead)
+        def _():
+            zt_load(1, p + 1).start()
+
+    @pl.loop(lead, pairs)
+    def _(p):
+        for d in range(2):
+            x_relay(p - lead, d, 1).wait_recv()
+        for d in range(2):
+            x_load(p, 1, d).start()
+        for d in range(2):
+            x_load(p, 0, d).wait()
+        vocab_step(p, 0, dz_a, dz_b, xbuf.at[1 - p % 2, 1], True)
+
+        @pl.when(p + 1 < pairs)
+        def _():
+            @pl.when(p + 1 >= lead + early)
             def _():
                 for d in range(2):
                     x_wait(p + 1 - lead, d)
                 for d in range(2):
                     x_relay(p + 1 - lead, d, 0).start()
-
-        @pl.when(p + 1 < pairs)
-        def _():
             for d in range(2):
                 x_load(p + 1, 0, d).start()
         for d in range(2):
             x_load(p, 1, d).wait()
-        vocab_step(p, 1, dz_b, dz_a, xbuf.at[p % 2, 0])
+        vocab_step(p, 1, dz_b, dz_a, xbuf.at[p % 2, 0], True)
 
     de_acc[...] += matmul(dz_b[...], xbuf[(pairs - 1) % 2, 1])
     de_out = pltpu.make_async_copy(de_acc, de_o, loc_sem.at[0])
@@ -461,9 +519,8 @@
             x_ring(j, d).wait_send()
             x_relay(j, d, 0).wait_send()
 
-    for t in range(tiles):
-        rows = pl.ds(t * TILE, TILE)
-        pltpu.make_async_copy(hid.at[rows, :], dh_o.at[rows, :], dh_sem.at[t]).wait()
+    for s in range(2):
+        dh_out(0, s).wait()
     de_out.wait()
 
 
@@ -487,25 +544,27 @@
                 sds((blocks, LANES), F32), sds((1, LANES), F32), sds((tokens, dim), BF16), sds((shard, dim), F32),
                 sds((1, dim), F32), sds((1, dim), F32),
                 sds((n * shard // PIECE, tiles, TILE, PIECE), F32), sds((n, tokens, dim), BF16),
+                sds((2, tiles, shard, TILE), F32),
             ),
             in_specs=[anywhere, vmem, vmem, anywhere, vmem, vmem],
-            out_specs=(vmem, vmem, anywhere, anywhere, vmem, vmem, anywhere, anywhere),
+            out_specs=(vmem, vmem, anywhere, anywhere, vmem, vmem, anywhere, anywhere, anywhere),
             scratch_shapes=[
                 pltpu.VMEM((n, shard, dim), BF16), pltpu.VMEM((tokens, dim), BF16), pltpu.VMEM((tokens, dim), BF16),
                 pltpu.VMEM((shard, dim), F32), pltpu.VMEM((tokens, LANES), F32), pltpu.VMEM((tokens, LANES), F32),
                 pltpu.VMEM((tokens, LANES), F32), pltpu.VMEM((tokens, LANES), F32),
                 pltpu.VMEM((2, 2, TILE, dim), BF16), pltpu.VMEM((shard, TILE), BF16), pltpu.VMEM((shard, TILE), BF16),
-                pltpu.VMEM((8, TILE, PIECE), F32), pltpu.VMEM((TILE, dim), F32), pltpu.VMEM((shard, TILE), F32),
-                pltpu.VMEM((TILE, LANES), F32), pltpu.VMEM((TILE, LANES), F32),
+                pltpu.VMEM((8, TILE, PIECE), F32), pltpu.VMEM((TILE, dim), F32), pltpu.VMEM((TILE, dim), F32),
+                pltpu.VMEM((TILE, dim), BF16), pltpu.VMEM((TILE, dim), BF16), pltpu.VMEM((shard, TILE), F32), pltpu.VMEM((shard, TILE), F32),
+                pltpu.VMEM((tokens, LANES), F32), pltpu.VMEM((tokens, LANES), F32),
                 pltpu.VMEM((n, blocks, LANES), jnp.int32), pltpu.VMEM((n, blocks, LANES), jnp.int32),
                 pltpu.VMEM((n, blocks, LANES), F32), pltpu.VMEM((n, 8, dim), F32), pltpu.VMEM((16, dim), F32),
                 pltpu.VMEM((8, LANES), F32),
                 dma((2, e_rounds)), dma((2, e_rounds)), dma((2, e_rounds)), dma((2, e_rounds)), dma((2,)),
                 dma((2, x_rounds)), dma((2, x_rounds)), dma((2, x_rounds)), dma((2, x_rounds)), dma((2,)),
                 dma((2, n)), dma((2, n)), dma((2, n)), dma((2, n)),
-                dma((tiles,)), dma((2,)), dma((2,)), dma((4, 2)), dma((2, 2)), dma((tiles,)),
+                dma((tiles,)), dma((2,)), dma((2,)), dma((2,)), dma((2, 2)), dma((2,)), dma((2,)), dma((2,)),
             ],
-            compiler_params=pltpu.CompilerParams(collective_id=0, has_side_effects=True, vmem_limit_bytes=60 * 1024 * 1024),
+            compiler_params=pltpu.CompilerParams(collective_id=0, has_side_effects=True, vmem_limit_bytes=63 * 1024 * 1024),
         )(hidden, ln_gain.reshape(1, dim), ln_bias.reshape(1, dim), embed, targets.reshape(blocks, LANES), loss_mask.reshape(blocks, LANES))
         loss, mean, d_hidden, d_embed, d_gain, d_bias = outs[:6]
         return loss.reshape(tokens), mean[0, :1], d_hidden, d_embed, d_gain.reshape(dim), d_bias.reshape(dim)

time: 265 us -> 257 us (0.970)
  Pallas kernels: 253 us -> 245 us
    pallas_call x1, Pallas kernels: 253 us -> 245 us  [body(): pl.pallas_call(functools.partial(kernel, n), out_shape=(sds((blocks, LANE...]
where the time goes in v3:
time: 257 us
  Pallas kernels  245 us (95%)
  local copies, waits for them, and re-layouts  9.33 us (4%)
    pallas_call x1, Pallas kernels, body(): pl.pallas_call(functools.partial(kernel, n), out_shape=(sds((blocks, LANE...  245 us
    unnamed x11, local copies, waits for them, and re-layouts  9.33 us

profile of v3, /device:TPU:81, one launch (start us, length us, event | category | flops | bytes accessed | tf_op | source)
XLA Modules:
  0.0 257.0 jit_solution(17350713036167935979)
XLA Ops:
  0.6 245.3 %shard_map.109 = (f32[16,128]{1,0:T(8,128)}, f32[1,128]{1,0:T(1,128)}, bf16[2048,1024]{1,0:T(8,128)(2,1)}, f32[1024,1024]{1,0:T(8,128)}, f32[1,1024]{1,0:T(1,128...) custom-call(bf16[2048,1024]{1,0:T(8,128)(2,1)} %hidden.1, ...), custom_call_target="tpu_custom_call" | custom-call | tf_op jit(solution)/shard_map/pallas_call | solution.py:541
  246.0 1.3 copy.18
  247.8 0.0 copy-start
  247.8 4.8 %copy.20 = bf16[2048,1024]{1,0:T(8,128)(2,1)} copy(bf16[2048,1024]{1,0:T(8,128)(2,1)} %get-tuple-element.26) | data formatting | bytes 8388608
  252.7 0.0 copy-done
  252.7 0.0 copy-start.2
  252.7 0.0 copy-start.1
  252.7 2.0 copy.21
  254.7 0.0 copy-done.2
  254.7 0.6 copy.22
  255.3 0.0 copy-done.1
  255.3 0.6 copy.23
Async XLA Ops:
  247.8 4.8 %copy-start = (f32[1024,1024]{1,0:T(8,128)S(1)}, f32[1024,1024]{1,0:T(8,128)}, u32[]{:S(2)}) copy-start(f32[1024,1024]{1,0:T(8,128)} %get-tuple-element.27) | copy-start | bytes 12582916
  252.7 2.0 copy-start.2
  252.7 2.6 %copy-start.1 = (f32[1,1024]{1,0:T(1,128)S(1)}, f32[1,1024]{1,0:T(1,128)}, u32[]{:S(2)}) copy-start(f32[1,1024]{1,0:T(1,128)} %get-tuple-element.17) | copy-start | bytes 12292

commit v4 on v3

--- a/solution.py
+++ b/solution.py
@@ -306,7 +306,7 @@
                 p = jnp.exp(z - lse)
                 top, at = g * LANES // TILE * TILE + b * LANES, (g * LANES) % TILE
                 out[top:top + LANES, at:at + LANES] = (jnp.where(hit, p - 1.0, p) * wc).astype(BF16)
-                found = found + jnp.where(hit, z, 0.0)
+                found = jnp.where(hit, z, found)
             sum_s[tok, :] = found
 
     def norm_back(t, at, count_rows, dx_ref, dh_ref):

time: 257 us -> 255 us (level)
  no operation moved by 1% of the time
where the time goes in v4:
time: 255 us
  Pallas kernels  243 us (95%)
  local copies, waits for them, and re-layouts  9.33 us (4%)
    pallas_call x1, Pallas kernels, body(): pl.pallas_call(functools.partial(kernel, n), out_shape=(sds((blocks, LANE...  243 us
    unnamed x11, local copies, waits for them, and re-layouts  9.33 us

profile of v4, /device:TPU:81, one launch (start us, length us, event | category | flops | bytes accessed | tf_op | source)
XLA Modules:
  0.0 254.5 jit_solution(4324303441456203462)
XLA Ops:
  0.6 242.8 %shard_map.109 = (f32[16,128]{1,0:T(8,128)}, f32[1,128]{1,0:T(1,128)}, bf16[2048,1024]{1,0:T(8,128)(2,1)}, f32[1024,1024]{1,0:T(8,128)}, f32[1,1024]{1,0:T(1,128...) custom-call(bf16[2048,1024]{1,0:T(8,128)(2,1)} %hidden.1, ...), custom_call_target="tpu_custom_call" | custom-call | tf_op jit(solution)/shard_map/pallas_call | solution.py:541
  243.5 1.3 copy.18
  245.3 0.0 copy-start
  245.3 4.8 %copy.20 = bf16[2048,1024]{1,0:T(8,128)(2,1)} copy(bf16[2048,1024]{1,0:T(8,128)(2,1)} %get-tuple-element.26) | data formatting | bytes 8388608
  250.2 0.0 copy-done
  250.2 0.0 copy-start.2
  250.2 0.0 copy-start.1
  250.2 2.0 copy.21
  252.2 0.0 copy-done.2
  252.2 0.6 copy.22
  252.8 0.0 copy-done.1
  252.8 0.6 copy.23
Async XLA Ops:
  245.3 4.8 %copy-start = (f32[1024,1024]{1,0:T(8,128)S(1)}, f32[1024,1024]{1,0:T(8,128)}, u32[]{:S(2)}) copy-start(f32[1024,1024]{1,0:T(8,128)} %get-tuple-element.27) | copy-start | bytes 12582916
  250.2 2.0 copy-start.2
  250.2 2.6 %copy-start.1 = (f32[1,1024]{1,0:T(1,128)S(1)}, f32[1,1024]{1,0:T(1,128)}, u32[]{:S(2)}) copy-start(f32[1,1024]{1,0:T(1,128)} %get-tuple-element.17) | copy-start | bytes 12292
